TPU v7x, 32 devices: a whole 2x2x4 slice. The times are simulated.
32 devices in a mesh: row: 8 (over z, x), col: 4 (over y, core).
Axes of the slice: x: 2, y: 2, z: 4, core: 2. Of those that a mesh axis runs over, the one named last changes fastest.
Arguments:
- gradients: bfloat16 [32, 1024, 5120], P(('row', 'col')), may hold values from -24 to 24
- bucket_lengths: int32 [16], replicated, may hold values from 1 to 128, 1024 in all
- owner_offset: int32 [8], replicated, may hold values from 0 to 3
- clip_rms: float32 [1], replicated, may hold values from 0.15 to 0.4
Outputs:
- clipped_shard: float32 [1024, 5120], P('row', 'col')
- bucket_rms: float32 [16], replicated
Inputs may be any that keep to these rules, and one draw needn't show every extreme that they name: `bucket_lengths`: the buckets cover all 1024 rows; the largest has exactly 128 rows.
All inputs are finite; a program needn't handle non-finite values.
Results may differ from a plain program's by a relative error of at most 0.0003.
Values sent between devices are 32-bit elements; how exact they have to be, the bound alone decides.
A program may use at most 128 MiB of HBM per device.

v0:
```python
import functools

import jax
import jax.numpy as jnp
from jax import lax
from jax.experimental import pallas as pl
from jax.experimental.pallas import tpu as pltpu
from jax.sharding import PartitionSpec as P

MESH = pl.DeviceIdType.MESH
F32 = jnp.float32
PARTS = 2
LAG = 2
ROWS = 16


def kernel(n_row, n_col, bits, g_ref, len_ref, off_ref, clip_ref, out_ref, rms_ref, src, send0, *rest):
    sums, rest = rest[: bits + 1], rest[bits + 1 :]
    mine, slots, sq, load_sem, sends, recvs, sa, ra = rest
    steps = send0.shape[0]
    blocks = 1 << bits
    devices = n_row * n_col
    _, rows, width = src.shape
    w = width // n_col
    part = w // PARTS
    row, col = lax.axis_index("row"), lax.axis_index("col")
    z, x = row // 2, row % 2
    y, core = col // 2, col % 2
    me = row * n_col + col

    def flip(value, bit):
        return value + (1 - 2 * ((value >> bit) % 2)) * (1 << bit)

    x_peer, y_peer = (flip(row, 0), col), (row, flip(col, 1))
    z_peers = [(flip(row, 1 + b), col) for b in range(bits - 2)]
    order = (
        [(row, flip(col, 0)), x_peer, z_peers[0], y_peer] + z_peers[1:],
        [(row, flip(col, 0)), y_peer, z_peers[0], x_peer] + z_peers[1:],
    )

    def place(k):
        other = (me + k) % devices
        return (other // n_col, other % n_col)

    def load(i):
        at = pl.ds(pl.multiple_of(i * ROWS, ROWS), ROWS)
        return pltpu.make_async_copy(g_ref.at[:, at], src.at[:, at], load_sem.at[i])

    def remote(a, b, s, r, dev):
        return pltpu.make_async_remote_copy(
            src_ref=a, dst_ref=b, send_sem=s, recv_sem=r, device_id=dev, device_id_type=MESH
        )

    def copy(stage, t, o):
        half = blocks >> stage
        a = send0.at[t, o] if stage == 0 else sums[stage - 1].at[t, o, pl.ds(half, half)]
        return remote(
            a, sums[stage].at[t, o], sends.at[stage, t, o], recvs.at[stage, t, o], order[o][stage]
        )

    def copya(k):
        return remote(mine, slots.at[me], sa.at[k], ra.at[me], place(k))

    @pl.loop(0, rows // ROWS)
    def _(i):
        load(i).start()

    barrier = pltpu.get_barrier_semaphore()

    @pl.loop(1, devices)
    def _(k):
        pl.semaphore_signal(barrier, inc=1, device_id=place(k), device_id_type=MESH)

    pl.semaphore_wait(barrier, devices - 1)

    def spot(i):
        xr, zr, yr = i >> (bits - 1), (i >> (bits - 2)) % 2, (i >> (bits - 3)) % 2
        low = i % (1 << (bits - 3))
        other = (
            (yr << (bits - 1)) + (zr << (bits - 2)) + (xr << (bits - 3)) + low
        )
        zd = (z + zr) % 2
        for b in range(1, bits - 2):
            zd = zd + ((((z >> b) + (low >> (bits - 3 - b))) % 2) << b)
        return zd * 2 + (x + xr) % 2, (y + yr) % 2, other

    def piece(t, r, c):
        at = pl.ds(pl.multiple_of((t // PARTS) * ROWS, ROWS), ROWS)
        origin = lax.rem(c + off_ref[r], n_col)
        total = None
        for j in range(n_col):
            gap = origin - j
            weight = jnp.maximum(1 - gap * gap, 0).astype(F32)
            begin = pl.multiple_of(j * w + (t % PARTS) * part, 128)
            term = src[r, at, pl.ds(begin, part)] * jnp.full((ROWS, part), weight, F32).astype(src.dtype)
            total = term if total is None else total + term
        return total.astype(F32)

    def convert(t):
        @pl.when(t % PARTS == 0)
        def _():
            load(t // PARTS).wait()

        @pl.loop(0, blocks, unroll=2)
        def _(i):
            r, yd, other = spot(i)
            v = piece(t, r, yd * 2 + 1 - core)
            send0[t, 0, i] = v[:8]
            send0[t, 1, other] = v[8:]

        for o in range(2):
            copy(0, t, o).start()

    def stage0(t):
        for o in range(2):
            copy(0, t, o).wait_recv()

        @pl.loop(0, blocks, unroll=2)
        def _(i):
            r, yd, other = spot(i)
            v = piece(t, r, yd * 2 + core)
            sums[0][t, 0, i] += v[:8]
            sums[0][t, 1, other] += v[8:]

        for o in range(2):
            copy(1, t, o).start()

    def fold(stage, t):
        for o in range(2):
            copy(stage, t, o).wait_recv()

            @pl.loop(0, blocks >> stage, unroll=2)
            def _(i):
                sums[stage][t, o, i] += sums[stage - 1][t, o, i]

            copy(stage + 1, t, o).start()

    def finish(t):
        for o in range(2):
            copy(bits, t, o).wait_recv()
            v = (sums[bits][t, o, 0] + sums[bits - 1][t, o, 0]) * (1.0 / devices)
            at = pl.ds(pl.multiple_of((t // PARTS) * ROWS + o * 8, 8), 8)
            out_ref[at, pl.ds(pl.multiple_of((t % PARTS) * part, 128), part)] = v
            v = v * v
            total = v[:, 0:128]
            for j in range(128, part, 128):
                total = total + v[:, j : j + 128]
            sq[t % PARTS, at, :] = total

    stages = [convert, stage0]
    stages += [functools.partial(fold, s) for s in range(1, bits)]
    stages += [finish]

    @pl.loop(0, steps + LAG * (len(stages) - 1))
    def _(t):
        for i, stage in enumerate(stages):
            lag = i * LAG

            @pl.when((t >= lag) & (t < steps + lag))
            def _():
                stage(t - lag)

    lane = lax.broadcasted_iota(jnp.int32, (1, 128), 1)
    starts = jnp.zeros((1, 128), jnp.int32)
    lengths = jnp.zeros((1, 128), jnp.int32)
    begin = jnp.int32(0)
    for b in range(len_ref.shape[0]):
        starts = jnp.where(lane == b, begin, starts)
        lengths = jnp.where(lane == b, len_ref[b], lengths)
        begin = begin + len_ref[b]
    ids = lax.broadcasted_iota(jnp.int32, (rows, 128), 0) + row * rows
    after = jnp.clip(ids - starts + 1, 0, 1)
    before = jnp.clip(starts + lengths - ids, 0, 1)
    inside = (after * before).astype(F32)
    row_squares = jnp.sum(jnp.sum(sq[...], axis=0), axis=1, keepdims=True)
    local = jnp.sum(inside * row_squares, axis=0, keepdims=True)
    mine[...] = local
    slots[me] = local

    @pl.loop(1, devices)
    def _(k):
        copya(k).start()

    @pl.loop(0, steps)
    def _(t):
        for o in range(2):
            for s in range(bits + 1):
                copy(s, t, o).wait_send()

    @pl.loop(1, devices)
    def _(k):
        other = (me + devices - k) % devices
        remote(mine, slots.at[other], sa.at[k], ra.at[other], place(k)).wait_recv()
        copya(k).wait_send()

    squares = slots[0]
    for i in range(1, devices):
        squares = squares + slots[i]
    overall = jnp.sqrt(jnp.sum(squares, axis=1, keepdims=True) / (n_row * rows * width))
    clip = clip_ref[0]
    factor = clip / jnp.maximum(overall, clip)
    out_ref[...] = out_ref[...] * factor
    rms = jnp.sqrt(squares / (jnp.maximum(lengths, 1).astype(F32) * width))
    rms_ref[...] = rms[:, : rms_ref.shape[1]]


def shards(n_row, n_col, gradients, bucket_lengths, owner_offset, clip_rms):
    _, total_rows, width = gradients.shape
    rows, w = total_rows // n_row, width // n_col
    devices = n_row * n_col
    steps = rows // ROWS * PARTS
    bits = devices.bit_length() - 2
    blocks = 1 << bits
    vmem, smem = pltpu.VMEM, pltpu.SMEM
    dma = pltpu.SemaphoreType.DMA
    clipped, rms = pl.pallas_call(
        functools.partial(kernel, n_row, n_col, bits),
        out_shape=(
            jax.ShapeDtypeStruct((rows, w), F32),
            jax.ShapeDtypeStruct((1, bucket_lengths.shape[0]), F32),
        ),
        in_specs=[
            pl.BlockSpec(memory_space=pl.ANY),
            pl.BlockSpec(memory_space=smem),
            pl.BlockSpec(memory_space=smem),
            pl.BlockSpec(memory_space=smem),
        ],
        out_specs=[pl.BlockSpec(memory_space=vmem)] * 2,
        scratch_shapes=[
            vmem((n_row, rows, width), gradients.dtype),
            vmem((steps, 2, blocks, 8, w // PARTS), F32),
            *[vmem((steps, 2, blocks >> s, 8, w // PARTS), F32) for s in range(bits + 1)],
            vmem((1, 128), F32),
            vmem((devices, 1, 128), F32),
            vmem((PARTS, rows, 128), F32),
            dma((rows // ROWS,)),
            dma((bits + 1, steps, 2)), dma((bits + 1, steps, 2)),
            dma((devices,)), dma((devices,)),
        ],
        compiler_params=pltpu.CompilerParams(
            collective_id=0, has_side_effects=True, vmem_limit_bytes=44 * 1024 * 1024
        ),
    )(gradients.reshape(n_row, rows, width), bucket_lengths, owner_offset, clip_rms)
    return clipped, rms[0]


def solution(mesh):
    n_row, n_col = mesh.shape["row"], mesh.shape["col"]
    in_specs = (P(("row", "col"), None, None), P(), P(), P())
    out_specs = (P("row", "col"), P())
    return jax.shard_map(
        functools.partial(shards, n_row, n_col),
        mesh=mesh, in_specs=in_specs, out_specs=out_specs, check_vma=False,
    )
```

profile of v0, /device:TPU:0, one launch (start us, length us, event | category | flops | bytes accessed | tf_op | source)
XLA Modules:
  0.0 103.6 jit_solution(18060449003131333409)
XLA Ops:
  1.3 0.0 copy-start
  1.3 0.6 copy-done
  1.9 0.0 copy-start.1
  1.9 0.7 copy-done.1
  2.6 99.6 %shard_map.59 = (f32[128,1280]{1,0:T(8,128)S(1)}, f32[1,16]{1,0:T(1,128)S(1)}) custom-call(bf16[8,128,5120]{2,1,0:T(8,128)(2,1)} %bitcast.3, s32[16]{0:T(128)S(1)} %copy-done, s32[8]{0:T(128)S(1)} %copy-done.1, f32[1]{0:T(128)S(6)} %copy.8.clip_ref), custom_call_target="tpu_custom_call" | custom-call | tf_op jit(solution)/shard_map/pallas_call | solution.py:216
  102.2 0.8 copy.9
  103.1 0.5 copy.10
Async XLA Ops:
  1.3 0.7 copy-start
  1.9 0.7 copy-start.1
where the time goes:
time: 104 us
  Pallas kernels  99.6 us (96%)
  local copies, waits for them, and re-layouts  2.65 us (3%)
  between operations  1.29 us (1%)
    pallas_call x1, Pallas kernels, shards(): pl.pallas_call(functools.partial(kernel, n_row, n_col, bits), out_shape=(...  99.6 us
    unnamed x6, local copies, waits for them, and re-layouts  2.65 us

commit v1 on v0

v1 whole, which is shorter than its diff:
```python
import functools

import jax
import jax.numpy as jnp
from jax import lax
from jax.experimental import pallas as pl
from jax.experimental.pallas import tpu as pltpu
from jax.sharding import PartitionSpec as P

MESH = pl.DeviceIdType.MESH
F32 = jnp.float32
ROWS = 16
COLS = 256
LANES = 3
INNER = 16
PARTS = 2
PLACES = (
    (1.08, 1.67, 1.70),
    (3.85, 3.82, 3.33),
    (6.25, 5.64, 6.04),
    (7.90, 7.35, 7.55),
    (10.61, 9.66, 10.24),
)


def plan(bits):
    places = list(PLACES[:4])
    while len(places) < bits:
        places.append(tuple(p + 1.5 for p in places[-1]))
    places.append(tuple(max(a, b + 1.5) for a, b in zip(PLACES[4], places[-1])))
    events = [(p % 1, s + 1, l, int(p // 1)) for s, row in enumerate(places) for l, p in enumerate(row)]
    spans = [[b - a for a, b in zip(x, y)] for x, y in zip([(0.0,) * LANES] + places, places)]
    rings = [max(2 * (int(d // 1) + 1) for d in row) for row in spans]
    return sorted(events), max(e[3] for e in events), rings


def kernel(n_row, n_col, bits, g_ref, len_hbm, off_hbm, clip_hbm, out_ref, stat_ref, src, head, *rest):
    sent, rest = rest[:LANES], rest[LANES:]
    sums, rest = [rest[l * (bits + 1) : (l + 1) * (bits + 1)] for l in range(LANES)], rest[LANES * (bits + 1) :]
    acc, bounds, mine, slots, len_ref, off_ref, clip_ref, load_sem, small_sem, *rest = rest
    sends, recvs, (both,) = rest[:LANES], rest[LANES : 2 * LANES], rest[2 * LANES :]
    events, deepest, rings = plan(bits)
    chunks = [s.shape[0] for s in sent]
    blocks = 1 << bits
    devices = n_row * n_col
    _, _, rows, w = src.shape
    width = w * n_col
    across = w // COLS
    row, col = lax.axis_index("row"), lax.axis_index("col")
    core = col % 2
    me = row * n_col + col
    small = [
        pltpu.make_async_copy(a, b, small_sem.at[i])
        for i, (a, b) in enumerate(((off_hbm, off_ref), (len_hbm, len_ref), (clip_hbm, clip_ref)))
    ]
    early = [
        pltpu.make_async_copy(g_ref.at[:, pl.ds(0, ROWS), pl.ds(j * w, LANES * COLS)], head.at[j], load_sem.at[j])
        for j in range(n_col)
    ]
    late = [
        pltpu.make_async_copy(g_ref.at[:, :, pl.ds(j * w, w)], src.at[j], load_sem.at[n_col + j])
        for j in range(n_col)
    ]
    for c in small[:1] + early + small[1:] + late:
        c.start()

    def turn(value, bit):
        return 1 - 2 * ((value >> bit) % 2)

    def flip(value, bit):
        return value + turn(value, bit) * (1 << bit)

    def peer(dim):
        return (row, flip(col, 1)) if dim == "y" else (flip(row, dim), col)

    high = list(range(2, bits - 1))
    orders = ([1, "xy", "yx"] + high, [0, "y", 1] + high, ["y", 0, 1] + high)

    def target(s, l, k):
        if s == 0:
            return (row, flip(col, 0))
        dim = orders[l][s - 1]
        if dim in ("xy", "yx"):
            pick = k % 2 if dim == "yx" else 1 - k % 2
            return (row + pick * turn(row, 0), col + (1 - pick) * turn(col, 1) * 2)
        return peer(dim)

    barrier = pltpu.get_barrier_semaphore()
    peers = [(row, flip(col, 0))] + [peer(d) for d in [0, "y", 1] + high]
    for other in peers:
        pl.semaphore_signal(barrier, inc=1, device_id=other, device_id_type=MESH)

    small[0].wait()

    def remote(a, b, s, r, dev):
        return pltpu.make_async_remote_copy(
            src_ref=a, dst_ref=b, send_sem=s, recv_sem=r, device_id=dev, device_id_type=MESH
        )

    def copy(s, l, k):
        half = blocks >> s
        a = sent[l].at[k] if s == 0 else sums[l][s - 1].at[k, pl.ds(half, half)]
        at = sum(rings[:s]) + k % rings[s]
        return remote(a, sums[l][s].at[k], sends[l].at[s], recvs[l].at[at], target(s, l, k))

    def unit(l, k):
        u = k * LANES + l
        return u, pl.multiple_of((u // across) * ROWS, ROWS), pl.multiple_of((u % across) * COLS, COLS)

    def spot(i, l, k):
        flips = {}
        for j, dim in enumerate(orders[l]):
            flips[dim] = (i >> (bits - 1 - j)) % 2
        if "xy" in flips:
            odd = k % 2
            flips[0] = flips["xy"] * (1 - odd) + flips["yx"] * odd
            flips["y"] = flips["yx"] * (1 - odd) + flips["xy"] * odd
        r = 0
        for b in range(bits - 1):
            r = r + (((row >> b) + flips[b]) % 2) * (1 << b)
        return r, (col // 2 + flips["y"]) % 2

    def each(lo, hi, fn):
        if hi - lo <= INNER:
            for i in range(lo, hi):
                fn(i)
        else:

            @pl.loop(0, (hi - lo) // INNER)
            def _(outer):
                for i in range(INNER):
                    fn(lo + outer * INNER + i)

    def piece(start, top, base, r, c, q):
        origin = lax.rem(c + off_ref[r], n_col)
        if start:
            return head[origin, r, :, pl.ds(base + q * 128, 128)].astype(F32)
        begin = pl.multiple_of(base + q * 128, 128)
        return src[origin, r, pl.ds(top, ROWS), pl.ds(begin, 128)].astype(F32)

    def convert(l, k, start=False):
        _, top, base = unit(l, k)
        base = l * COLS if start else base

        def fill(i):
            r, yd = spot(i, l, k)
            for q in range(COLS // 128):
                sent[l][k, i, :, q * 128 : (q + 1) * 128] = piece(start, top, base, r, yd * 2 + 1 - core, q)

        each(0, blocks, fill)

    def first(l, k, start=False):
        copy(0, l, k).wait_recv()
        _, top, base = unit(l, k)
        base = l * COLS if start else base

        def fold(i):
            r, yd = spot(i, l, k)
            for q in range(COLS // 128):
                sums[l][0][k, i, :, q * 128 : (q + 1) * 128] += piece(start, top, base, r, yd * 2 + core, q)

        each(blocks // 2, blocks, fold)
        copy(1, l, k).start()
        each(0, blocks // 2, fold)

    def middle(s, l, k):
        copy(s - 1, l, k).wait_recv()
        half = blocks >> s

        @pl.loop(half, 2 * half, unroll=min(2, half))
        def _(i):
            sums[l][s - 1][k, i] += sums[l][s - 2][k, i]

        copy(s, l, k).start()

        @pl.loop(0, half, unroll=min(2, half))
        def _(i):
            sums[l][s - 1][k, i] += sums[l][s - 2][k, i]

    def finish(l, k):
        copy(bits, l, k).wait_recv()
        _, top, base = unit(l, k)
        v = (sums[l][bits][k, 0] + sums[l][bits - 1][k, 0]) * (1.0 / devices)
        out_ref[pl.ds(top, ROWS), pl.ds(base, COLS)] = v
        v = v * v
        total = v[:, 0:128]
        for q in range(128, COLS, 128):
            total = total + v[:, q : q + 128]
        ids = lax.broadcasted_iota(jnp.int32, (ROWS, 128), 0) + row * rows + top
        after = jnp.clip(ids - bounds[0] + 1, 0, 1)
        before = jnp.clip(bounds[1] - ids, 0, 1)
        acc[...] += (after * before).astype(F32) * jnp.sum(total, axis=1, keepdims=True)

    def step(s, l, k):
        if s == 1:
            first(l, k)
        elif s <= bits:
            middle(s, l, k)
        else:
            finish(l, k)

    for c in early:
        c.wait()
    for l in range(LANES):
        convert(l, 0, True)

    small[1].wait()
    small[2].wait()
    lane = lax.broadcasted_iota(jnp.int32, (1, 128), 1)
    starts = jnp.zeros((1, 128), jnp.int32)
    lengths = jnp.zeros((1, 128), jnp.int32)
    begin = jnp.int32(0)
    for b in range(len_ref.shape[0]):
        starts = jnp.where(lane == b, begin, starts)
        lengths = jnp.where(lane == b, len_ref[b], lengths)
        begin = begin + len_ref[b]
    bounds[0] = starts
    bounds[1] = starts + lengths
    bounds[2] = lengths
    acc[...] = jnp.zeros_like(acc)

    pl.semaphore_wait(barrier, len(peers))
    for l in range(LANES):
        copy(0, l, 0).start()
    for l in range(LANES):
        first(l, 0, True)
    for c in late:
        c.wait()

    @pl.loop(1, chunks[0] + deepest)
    def _(t):
        for l in range(LANES):

            @pl.when(t < chunks[l])
            def _():
                convert(l, t)
                copy(0, l, t).start()

        for _, s, l, lag in events:

            @pl.when((t >= lag + (1 if s == 1 else 0)) & (t < chunks[l] + lag))
            def _():
                step(s, l, t - lag)

    local = jnp.sum(acc[...], axis=0, keepdims=True)
    mine[...] = local
    slots[me] = local

    def share(mask):
        other = me
        for b in range(bits + 1):
            if (mask >> b) % 2:
                other = flip(other, b)
        return remote(mine, slots.at[me], both.at[0], both.at[1], (other // n_col, other % n_col))

    for mask in range(devices - 1, 0, -1):
        share(mask).start()

    for l in range(LANES):
        for s in range(bits + 1):
            half = blocks >> s
            a = sent[l] if s == 0 else sums[l][s - 1].at[:, pl.ds(half, half)]
            pltpu.make_async_copy(a, a, sends[l].at[s]).wait()

    others = slots.at[pl.ds(0, devices - 1)]
    pltpu.make_async_copy(others, others, both.at[1]).wait()

    squares = slots[0]
    for i in range(1, devices):
        squares = squares + slots[i]
    overall = jnp.sqrt(jnp.sum(squares, axis=1, keepdims=True) / (n_row * rows * width))
    clip = clip_ref[0]
    factor = clip / jnp.maximum(overall, clip)
    rms = jnp.sqrt(squares / (jnp.maximum(bounds[2], 1).astype(F32) * width))
    stat_ref[0] = jnp.broadcast_to(factor, (8, 128))
    stat_ref[1] = jnp.broadcast_to(rms, (8, 128))
    pltpu.make_async_copy(others, others, both.at[0]).wait()


def scale(avg_ref, stat_ref, out_hbm, rms_hbm, out, rms, sem):
    rms[...] = stat_ref[1, 0:1, : rms.shape[1]]
    last = pltpu.make_async_copy(rms, rms_hbm, sem.at[0])
    last.start()
    factor = stat_ref[0, 0:1, 0:1]
    part = avg_ref.shape[0] // PARTS
    copies = []
    for i in range(PARTS):
        at = pl.ds(i * part, part)
        out[at] = avg_ref[at] * factor
        copies.append(pltpu.make_async_copy(out.at[at], out_hbm.at[at], sem.at[i + 1]))
        copies[-1].start()
    for c in copies:
        c.wait()
    last.wait()


def shards(n_row, n_col, gradients, bucket_lengths, owner_offset, clip_rms):
    _, total_rows, width = gradients.shape
    rows, w = total_rows // n_row, width // n_col
    devices = n_row * n_col
    bits = devices.bit_length() - 2
    blocks = 1 << bits
    units = rows // ROWS * (w // COLS)
    chunks = [(units - l + LANES - 1) // LANES for l in range(LANES)]
    vmem, smem = pltpu.VMEM, pltpu.SMEM
    dma = pltpu.SemaphoreType.DMA
    averaged, stats = pl.pallas_call(
        functools.partial(kernel, n_row, n_col, bits),
        out_shape=(
            jax.ShapeDtypeStruct((rows, w), F32),
            jax.ShapeDtypeStruct((2, 8, 128), F32),
        ),
        in_specs=[pl.BlockSpec(memory_space=pltpu.HBM)] * 4,
        out_specs=[pl.BlockSpec(memory_space=vmem)] * 2,
        scratch_shapes=[
            vmem((n_col, n_row, rows, w), gradients.dtype),
            vmem((n_col, n_row, ROWS, LANES * COLS), gradients.dtype),
            *[vmem((k, blocks, ROWS, COLS), F32) for k in chunks],
            *[vmem((k, blocks >> s, ROWS, COLS), F32) for k in chunks for s in range(bits + 1)],
            vmem((ROWS, 128), F32),
            vmem((3, 1, 128), jnp.int32),
            vmem((1, 128), F32),
            vmem((devices, 1, 128), F32),
            smem(bucket_lengths.shape, jnp.int32),
            smem(owner_offset.shape, jnp.int32),
            smem(clip_rms.shape, F32),
            dma((2 * n_col,)),
            dma((3,)),
            *[dma((bits + 1,)) for _ in chunks],
            *[dma((sum(plan(bits)[2]),)) for _ in chunks],
            dma((2,)),
        ],
        compiler_params=pltpu.CompilerParams(
            collective_id=0, has_side_effects=True, vmem_limit_bytes=50 * 1024 * 1024
        ),
    )(gradients.reshape(n_row, rows, width), bucket_lengths, owner_offset, clip_rms)
    count = bucket_lengths.shape[0]
    clipped, rms = pl.pallas_call(
        scale,
        out_shape=(jax.ShapeDtypeStruct((rows, w), F32), jax.ShapeDtypeStruct((1, count), F32)),
        in_specs=[pl.BlockSpec(memory_space=vmem)] * 2,
        out_specs=[pl.BlockSpec(memory_space=pltpu.HBM)] * 2,
        scratch_shapes=[vmem((rows, w), F32), vmem((1, count), F32), dma((PARTS + 1,))],
        compiler_params=pltpu.CompilerParams(vmem_limit_bytes=4 * 1024 * 1024),
    )(averaged, stats)
    return clipped, rms[0]


def solution(mesh):
    n_row, n_col = mesh.shape["row"], mesh.shape["col"]
    in_specs = (P(("row", "col"), None, None), P(), P(), P())
    out_specs = (P("row", "col"), P())
    return jax.shard_map(
        functools.partial(shards, n_row, n_col),
        mesh=mesh, in_specs=in_specs, out_specs=out_specs, check_vma=False,
    )
```

time: 104 us -> 94.3 us (0.907)
  Pallas kernels: 99.6 us -> 91.5 us
  local copies, waits for them, and re-layouts: 2.65 us -> 1.3 us
    pallas_call x1, Pallas kernels: 99.6 us -> 90.6 us  [shards(): pl.pallas_call(functools.partial(kernel, n_row, n_col, bits), out_shape=(...]
    unnamed x6 -> x4, local copies, waits for them, and re-layouts: 2.65 us -> 1.3 us
where the time goes in v1:
time: 94.3 us; the launch traced here: 94.1 us
  Pallas kernels  91.5 us (97%)
  local copies, waits for them, and re-layouts  1.3 us (1%)
  between operations  1.29 us (1%)
    pallas_call x1, Pallas kernels, shards(): pl.pallas_call(functools.partial(kernel, n_row, n_col, bits), out_shape=(...  90.6 us

profile of v1, /device:TPU:0, one launch (start us, length us, event | category | flops | bytes accessed | tf_op | source)
XLA Modules:
  0.0 94.1 jit_solution(14075635093163795643)
XLA Ops:
  1.3 0.0 copy-start
  1.3 0.6 copy-done
  1.9 0.0 copy-start.1
  1.9 0.7 copy-done.1
  2.6 90.6 %shard_map.59 = (f32[128,1280]{1,0:T(8,128)S(1)}, f32[2,8,128]{2,1,0:T(8,128)S(1)}) custom-call(bf16[8,128,5120]{2,1,0:T(8,128)(2,1)} %bitcast.2, s32[16]{0:T(128)S(1)} %copy-done, s32[8]{0:T(128)S(1)} %copy-done.1, f32[1]{0:T(128)S(6)} %copy.6.clip_hbm), custom_call_target="tpu_custom_call" | custom-call | tf_op jit(solution)/shard_map/pallas_call | solution.py:307
  93.2 0.9 shard_map.60
Async XLA Ops:
  1.3 0.7 copy-start
  1.9 0.7 copy-start.1

commit v2 on v1

v2 whole, which is shorter than its diff:
```python
import functools

import jax
import jax.numpy as jnp
from jax import lax
from jax.experimental import pallas as pl
from jax.experimental.pallas import tpu as pltpu
from jax.sharding import PartitionSpec as P

MESH = pl.DeviceIdType.MESH
F32 = jnp.float32
ROWS = 16
COLS = 256
LANES = 3
PARTS = 2
INNER = 16
PLACES = (
    (1.08, 1.67, 1.70),
    (3.85, 3.82, 3.33),
    (6.25, 5.64, 6.04),
    (7.90, 7.35, 7.55),
    (10.61, 9.66, 10.24),
)


def split(units):
    even = units * 13 // 40
    return [units - 2 * even, even, even]


def plan(bits):
    places = list(PLACES[:4])
    while len(places) < bits:
        places.append(tuple(p + 1.5 for p in places[-1]))
    places.append(tuple(max(a, b + 1.5) for a, b in zip(PLACES[4], places[-1])))
    events = [(p % 1, s + 1, l, int(p // 1)) for s, row in enumerate(places) for l, p in enumerate(row)]
    spans = [[b - a for a, b in zip(x, y)] for x, y in zip([(0.0,) * LANES] + places, places)]
    rings = [[2 * (int(row[l] // 1) + 1) for row in spans] for l in range(LANES)]
    return sorted(events), rings


def kernel(n_row, n_col, bits, g_ref, off_hbm, out_ref, stat_ref, src, head, *rest):
    sent, rest = rest[:LANES], rest[LANES:]
    sums, rest = [rest[l * (bits + 1) : (l + 1) * (bits + 1)] for l in range(LANES)], rest[LANES * (bits + 1) :]
    acc, mine, slots, off_ref, load_sem, *rest = rest
    sends, recvs, (both,) = rest[:LANES], rest[LANES : 2 * LANES], rest[2 * LANES :]
    events, rings = plan(bits)
    chunks = [s.shape[0] for s in sent]
    blocks = 1 << bits
    devices = n_row * n_col
    _, _, rows, w = src.shape
    width = w * n_col
    across = w // COLS
    row, col = lax.axis_index("row"), lax.axis_index("col")
    core = col % 2
    me = row * n_col + col
    bases = [sum(chunks[:l]) for l in range(LANES)]

    def unit(l, k):
        u = bases[l] + k
        return (u // across) * ROWS, (u % across) * COLS

    small = pltpu.make_async_copy(off_hbm, off_ref, load_sem.at[2])
    small.start()
    for l in range(LANES):
        top, base = unit(l, 0)
        for j in range(n_col):
            part = g_ref.at[:, pl.ds(top, ROWS), pl.ds(j * w + base, COLS)]
            pltpu.make_async_copy(part, head.at[l, j], load_sem.at[0]).start()
    for j in range(n_col):
        pltpu.make_async_copy(g_ref.at[:, :, pl.ds(j * w, w)], src.at[j], load_sem.at[1]).start()

    def turn(value, bit):
        return 1 - 2 * ((value >> bit) % 2)

    def flip(value, bit):
        return value + turn(value, bit) * (1 << bit)

    def peer(dim):
        return (row, flip(col, 1)) if dim == "y" else (flip(row, dim), col)

    high = list(range(2, bits - 1))
    orders = ([1, "xy", "yx"] + high, [0, "y", 1] + high, ["y", 0, 1] + high)

    def target(s, l, k):
        if s == 0:
            return (row, flip(col, 0))
        dim = orders[l][s - 1]
        if dim in ("xy", "yx"):
            pick = k % 2 if dim == "yx" else 1 - k % 2
            return (row + pick * turn(row, 0), col + (1 - pick) * turn(col, 1) * 2)
        return peer(dim)

    barrier = pltpu.get_barrier_semaphore()
    peers = [(row, flip(col, 0))] + [peer(d) for d in [0, "y", 1] + high]
    for other in peers:
        pl.semaphore_signal(barrier, inc=1, device_id=other, device_id_type=MESH)

    def remote(a, b, s, r, dev):
        return pltpu.make_async_remote_copy(
            src_ref=a, dst_ref=b, send_sem=s, recv_sem=r, device_id=dev, device_id_type=MESH
        )

    def copy(s, l, k):
        half = blocks >> s
        a = sent[l].at[k] if s == 0 else sums[l][s - 1].at[k, pl.ds(half, half)]
        at = sum(rings[l][:s]) + k % rings[l][s]
        return remote(a, sums[l][s].at[k], sends[l].at[s], recvs[l].at[at], target(s, l, k))

    def spot(i, l, k):
        flips = {}
        for j, dim in enumerate(orders[l]):
            flips[dim] = (i >> (bits - 1 - j)) % 2
        if "xy" in flips:
            odd = k % 2
            flips[0] = flips["xy"] * (1 - odd) + flips["yx"] * odd
            flips["y"] = flips["yx"] * (1 - odd) + flips["xy"] * odd
        r = 0
        for b in range(bits - 1):
            r = r + (((row >> b) + flips[b]) % 2) * (1 << b)
        return r, (col // 2 + flips["y"]) % 2

    def each(lo, hi, fn):
        if hi - lo <= INNER:
            for i in range(lo, hi):
                fn(i)
        else:

            @pl.loop(0, (hi - lo) // INNER)
            def _(outer):
                for i in range(INNER):
                    fn(lo + outer * INNER + i)

    def piece(l, k, start, r, c, q):
        origin = lax.rem(c + off_ref[r], n_col)
        if start:
            return head[l, origin, r, :, q * 128 : (q + 1) * 128].astype(F32)
        top, base = unit(l, k)
        at = pl.ds(pl.multiple_of(top, ROWS), ROWS)
        return src[origin, r, at, pl.ds(pl.multiple_of(base + q * 128, 128), 128)].astype(F32)

    def convert(l, k, start=False):
        def fill(i):
            r, yd = spot(i, l, k)
            for q in range(COLS // 128):
                sent[l][k, i, :, q * 128 : (q + 1) * 128] = piece(l, k, start, r, yd * 2 + 1 - core, q)

        each(0, blocks, fill)

    def first(l, k, start=False):
        copy(0, l, k).wait_recv()

        def fold(i):
            r, yd = spot(i, l, k)
            for q in range(COLS // 128):
                sums[l][0][k, i, :, q * 128 : (q + 1) * 128] += piece(l, k, start, r, yd * 2 + core, q)

        each(blocks // 2, blocks, fold)
        copy(1, l, k).start()
        each(0, blocks // 2, fold)

    def middle(s, l, k):
        copy(s - 1, l, k).wait_recv()
        half = blocks >> s

        @pl.loop(half, 2 * half, unroll=min(2, half))
        def _(i):
            sums[l][s - 1][k, i] += sums[l][s - 2][k, i]

        copy(s, l, k).start()

        @pl.loop(0, half, unroll=min(2, half))
        def _(i):
            sums[l][s - 1][k, i] += sums[l][s - 2][k, i]

    def finish(l, k):
        copy(bits, l, k).wait_recv()
        top, base = unit(l, k)
        v = (sums[l][bits][k, 0] + sums[l][bits - 1][k, 0]) * (1.0 / devices)
        out_ref[pl.ds(pl.multiple_of(top, ROWS), ROWS), pl.ds(pl.multiple_of(base, COLS), COLS)] = v
        v = v * v
        total = v[:, 0:128]
        for q in range(128, COLS, 128):
            total = total + v[:, q : q + 128]
        here = lax.broadcasted_iota(jnp.int32, acc.shape, 0) + top
        lane = lax.broadcasted_iota(jnp.int32, acc.shape, 1)
        acc[...] += jnp.where(here == lane, jnp.sum(total, axis=1, keepdims=True), 0.0)

    def step(s, l, k):
        if s == 1:
            first(l, k)
        elif s <= bits:
            middle(s, l, k)
        else:
            finish(l, k)

    acc[...] = jnp.zeros_like(acc)
    small.wait()
    pltpu.make_async_copy(head, head, load_sem.at[0]).wait()
    for l in range(LANES):
        convert(l, 0, True)
    pl.semaphore_wait(barrier, len(peers))
    for l in range(LANES):
        copy(0, l, 0).start()
    for l in range(LANES):
        first(l, 0, True)
    pltpu.make_async_copy(src, src, load_sem.at[1]).wait()

    @pl.loop(1, max(chunks[l] + lag for _, _, l, lag in events))
    def _(t):
        for l in range(LANES):

            @pl.when(t < chunks[l])
            def _():
                convert(l, t)
                copy(0, l, t).start()

        for _, s, l, lag in events:

            @pl.when((t >= lag + (1 if s == 1 else 0)) & (t < chunks[l] + lag))
            def _():
                step(s, l, t - lag)

    local = jnp.sum(acc[...], axis=0, keepdims=True)
    mine[...] = local
    slots[me] = local

    def share(mask):
        other = me
        for b in range(bits + 1):
            if (mask >> b) % 2:
                other = flip(other, b)
        return remote(mine, slots.at[me], both.at[0], both.at[1], (other // n_col, other % n_col))

    for mask in range(devices - 1, 0, -1):
        share(mask).start()

    for l in range(LANES):
        for s in range(bits + 1):
            half = blocks >> s
            a = sent[l] if s == 0 else sums[l][s - 1].at[:, pl.ds(half, half)]
            pltpu.make_async_copy(a, a, sends[l].at[s]).wait()

    others = slots.at[pl.ds(0, devices - 1)]
    pltpu.make_async_copy(others, others, both.at[1]).wait()

    for r in range(n_row):
        total = slots[r * n_col]
        for c in range(1, n_col):
            total = total + slots[r * n_col + c]
        stat_ref[pl.ds(r, 1)] = total
    pltpu.make_async_copy(others, others, both.at[0]).wait()


def scale(devices, avg_ref, stat_ref, len_ref, clip_ref, out_hbm, rms_hbm, out, rms, sem):
    rows, w = avg_ref.shape
    n_row, wide = stat_ref.shape
    count = len_ref.shape[1]
    stat = stat_ref[...]
    total = jnp.sum(jnp.sum(stat, axis=0, keepdims=True), axis=1, keepdims=True)
    overall = jnp.sqrt(total / (devices * rows * w))
    clip = clip_ref[0]
    factor = clip / jnp.maximum(overall, clip)
    part = rows // PARTS
    copies = []
    for i in range(PARTS):
        at = pl.ds(i * part, part)
        out[at] = avg_ref[at] * factor
        copies.append(pltpu.make_async_copy(out.at[at], out_hbm.at[at], sem.at[i + 1]))
        copies[-1].start()
    one = lax.broadcasted_iota(jnp.int32, (count, count), 0)
    two = lax.broadcasted_iota(jnp.int32, (count, count), 1)
    lengths = jnp.broadcast_to(len_ref[...].astype(F32), (count, count))
    ends = jnp.sum(jnp.where(two <= one, lengths, 0.0), axis=1, keepdims=True)
    size = jnp.sum(jnp.where(two == one, lengths, 0.0), axis=1, keepdims=True)
    lane = lax.broadcasted_iota(jnp.int32, (count, wide), 1)
    inside = jnp.zeros((count, wide), F32)
    for r in range(n_row):
        ids = (lane + r * rows).astype(F32)
        inside = inside + jnp.where((ids >= ends - size) & (ids < ends), stat[r : r + 1], 0.0)
    squares = jnp.sum(inside, axis=1, keepdims=True)
    column = jnp.sqrt(squares / (jnp.maximum(size, 1.0) * (w * devices // n_row)))
    rms[...] = jnp.sum(jnp.where(two == one, column, 0.0), axis=0, keepdims=True)
    copies.append(pltpu.make_async_copy(rms, rms_hbm, sem.at[0]))
    copies[-1].start()
    for c in copies:
        c.wait()


def shards(n_row, n_col, gradients, bucket_lengths, owner_offset, clip_rms):
    _, total_rows, width = gradients.shape
    rows, w = total_rows // n_row, width // n_col
    devices = n_row * n_col
    bits = devices.bit_length() - 2
    blocks = 1 << bits
    units = rows // ROWS * (w // COLS)
    chunks = split(units)
    wide = -(-rows // 128) * 128
    vmem, smem = pltpu.VMEM, pltpu.SMEM
    dma = pltpu.SemaphoreType.DMA
    averaged, stats = pl.pallas_call(
        functools.partial(kernel, n_row, n_col, bits),
        out_shape=(
            jax.ShapeDtypeStruct((rows, w), F32),
            jax.ShapeDtypeStruct((n_row, wide), F32),
        ),
        in_specs=[pl.BlockSpec(memory_space=pltpu.HBM)] * 2,
        out_specs=[pl.BlockSpec(memory_space=vmem)] * 2,
        scratch_shapes=[
            vmem((n_col, n_row, rows, w), gradients.dtype),
            vmem((LANES, n_col, n_row, ROWS, COLS), gradients.dtype),
            *[vmem((k, blocks, ROWS, COLS), F32) for k in chunks],
            *[vmem((k, blocks >> s, ROWS, COLS), F32) for k in chunks for s in range(bits + 1)],
            vmem((ROWS, wide), F32),
            vmem((1, wide), F32),
            vmem((devices, 1, wide), F32),
            smem(owner_offset.shape, jnp.int32),
            dma((3,)),
            *[dma((bits + 1,)) for _ in chunks],
            *[dma((sum(ring),)) for ring in plan(bits)[1]],
            dma((2,)),
        ],
        compiler_params=pltpu.CompilerParams(
            collective_id=0, has_side_effects=True, vmem_limit_bytes=50 * 1024 * 1024
        ),
    )(gradients.reshape(n_row, rows, width), owner_offset)
    count = bucket_lengths.shape[0]
    clipped, rms = pl.pallas_call(
        functools.partial(scale, devices),
        out_shape=(jax.ShapeDtypeStruct((rows, w), F32), jax.ShapeDtypeStruct((1, count), F32)),
        in_specs=[pl.BlockSpec(memory_space=m) for m in (vmem, vmem, vmem, smem)],
        out_specs=[pl.BlockSpec(memory_space=pltpu.HBM)] * 2,
        scratch_shapes=[vmem((rows, w), F32), vmem((1, count), F32), dma((PARTS + 1,))],
        compiler_params=pltpu.CompilerParams(vmem_limit_bytes=4 * 1024 * 1024),
    )(averaged, stats, bucket_lengths.reshape(1, count), clip_rms)
    return clipped, rms[0]


def solution(mesh):
    n_row, n_col = mesh.shape["row"], mesh.shape["col"]
    in_specs = (P(("row", "col"), None, None), P(), P(), P())
    out_specs = (P("row", "col"), P())
    return jax.shard_map(
        functools.partial(shards, n_row, n_col),
        mesh=mesh, in_specs=in_specs, out_specs=out_specs, check_vma=False,
    )
```

time: 94.3 us -> 93.5 us (level)
  no operation moved by 1% of the time
where the time goes in v2:
time: 93.5 us; the launch traced here: 93.3 us
  Pallas kernels  91.3 us (98%)
  between operations  1.32 us (1%)
    pallas_call x1, Pallas kernels, shards(): pl.pallas_call(functools.partial(kernel, n_row, n_col, bits), out_shape=(...  90.3 us

profile of v2, /device:TPU:0, one launch (start us, length us, event | category | flops | bytes accessed | tf_op | source)
XLA Modules:
  0.0 93.3 jit_solution(2732147173839105109)
XLA Ops:
  0.6 0.0 copy-start
  1.3 0.0 copy-start.1
  1.3 0.6 copy-done.1
  2.0 90.3 %shard_map.59 = (f32[128,1280]{1,0:T(8,128)S(1)}, f32[8,128]{1,0:T(8,128)S(1)}) custom-call(bf16[8,128,5120]{2,1,0:T(8,128)(2,1)} %bitcast.4, s32[8]{0:T(128)S(1)} %copy-done.1), custom_call_target="tpu_custom_call" | custom-call | tf_op jit(solution)/shard_map/pallas_call | solution.py:301
  92.3 0.0 copy-done
  92.3 1.0 %shard_map.60 = (f32[128,1280]{1,0:T(8,128)}, f32[1,16]{1,0:T(1,128)}) custom-call(f32[128,1280]{1,0:T(8,128)S(1)} %get-tuple-element.6.avg_ref, f32[8,128]{1,0:T(8,128)S(1)} %get-tuple-element.7.stat_ref, s32[1,16]{1,0:T(1,128)S(1)} %bitcast.3, f32[1]{0:T(128)S(6)} %copy.6.clip_ref), custom_call_target="tpu_custom_call" | custom-call | tf_op jit(solution)/shard_map/pallas_call | solution.py:328
Async XLA Ops:
  0.6 91.7 %copy-start = (s32[16]{0:T(128)S(1)}, s32[16]{0:T(128)}, u32[]{:S(2)}) copy-start(s32[16]{0:T(128)} %param.5) | copy-start | bytes 196
  1.3 0.7 copy-start.1

commit v3 on v2

--- a/solution.py
+++ b/solution.py
@@ -12,7 +12,8 @@
 ROWS = 16
 COLS = 256
 LANES = 3
-PARTS = 2
+PARTS = 1
+EARLY = 2
 INNER = 16
 PLACES = (
     (1.08, 1.67, 1.70),
@@ -39,10 +40,11 @@
     return sorted(events), rings
 
 
-def kernel(n_row, n_col, bits, g_ref, off_hbm, out_ref, stat_ref, src, head, *rest):
+def kernel(n_row, n_col, bits, g_ref, off_hbm, out_ref, stat_ref, src, *rest):
+    head, rest = rest[:EARLY], rest[EARLY:]
     sent, rest = rest[:LANES], rest[LANES:]
     sums, rest = [rest[l * (bits + 1) : (l + 1) * (bits + 1)] for l in range(LANES)], rest[LANES * (bits + 1) :]
-    acc, mine, slots, off_ref, load_sem, *rest = rest
+    acc, mine, slots, off_ref, load_sem, begin, *rest = rest
     sends, recvs, (both,) = rest[:LANES], rest[LANES : 2 * LANES], rest[2 * LANES :]
     events, rings = plan(bits)
     chunks = [s.shape[0] for s in sent]
@@ -60,13 +62,14 @@
         u = bases[l] + k
         return (u // across) * ROWS, (u % across) * COLS
 
-    small = pltpu.make_async_copy(off_hbm, off_ref, load_sem.at[2])
+    small = pltpu.make_async_copy(off_hbm, off_ref, load_sem.at[0])
     small.start()
-    for l in range(LANES):
-        top, base = unit(l, 0)
-        for j in range(n_col):
-            part = g_ref.at[:, pl.ds(top, ROWS), pl.ds(j * w + base, COLS)]
-            pltpu.make_async_copy(part, head.at[l, j], load_sem.at[0]).start()
+    for k in range(EARLY):
+        for l in range(LANES):
+            top, base = unit(l, k)
+            for j in range(n_col):
+                part = g_ref.at[:, pl.ds(top, ROWS), pl.ds(j * w + base, COLS)]
+                pltpu.make_async_copy(part, head[k].at[l, j], load_sem.at[2 + k]).start()
     for j in range(n_col):
         pltpu.make_async_copy(g_ref.at[:, :, pl.ds(j * w, w)], src.at[j], load_sem.at[1]).start()
 
@@ -134,21 +137,32 @@
     def piece(l, k, start, r, c, q):
         origin = lax.rem(c + off_ref[r], n_col)
         if start:
-            return head[l, origin, r, :, q * 128 : (q + 1) * 128].astype(F32)
+            return head[k][l, origin, r, :, q * 128 : (q + 1) * 128].astype(F32)
         top, base = unit(l, k)
         at = pl.ds(pl.multiple_of(top, ROWS), ROWS)
         return src[origin, r, at, pl.ds(pl.multiple_of(base + q * 128, 128), 128)].astype(F32)
 
-    def convert(l, k, start=False):
+    def convert(l, k, start=False, lo=0, hi=blocks):
         def fill(i):
             r, yd = spot(i, l, k)
             for q in range(COLS // 128):
                 sent[l][k, i, :, q * 128 : (q + 1) * 128] = piece(l, k, start, r, yd * 2 + 1 - core, q)
 
-        each(0, blocks, fill)
+        each(lo, hi, fill)
+
+    def halves(l):
+        half = blocks // 2
+        parts = ((half, begin.at[l]), (0, recvs[l].at[0]))
+        return [
+            remote(sent[l].at[0, pl.ds(at, half)], sums[l][0].at[0, pl.ds(at, half)], sends[l].at[0], sem, target(0, l, 0))
+            for at, sem in parts
+        ]
 
     def first(l, k, start=False):
-        copy(0, l, k).wait_recv()
+        if start and k == 0:
+            halves(l)[0].wait_recv()
+        else:
+            copy(0, l, k).wait_recv()
 
         def fold(i):
             r, yd = spot(i, l, k)
@@ -157,6 +171,8 @@
 
         each(blocks // 2, blocks, fold)
         copy(1, l, k).start()
+        if start and k == 0:
+            halves(l)[1].wait_recv()
         each(0, blocks // 2, fold)
 
     def middle(s, l, k):
@@ -196,17 +212,23 @@
 
     acc[...] = jnp.zeros_like(acc)
     small.wait()
-    pltpu.make_async_copy(head, head, load_sem.at[0]).wait()
-    for l in range(LANES):
-        convert(l, 0, True)
     pl.semaphore_wait(barrier, len(peers))
-    for l in range(LANES):
-        copy(0, l, 0).start()
-    for l in range(LANES):
-        first(l, 0, True)
+    pltpu.make_async_copy(head[0], head[0], load_sem.at[2]).wait()
+    for part, lo in enumerate((blocks // 2, 0)):
+        for l in range(LANES):
+            convert(l, 0, True, lo, lo + blocks // 2)
+            halves(l)[part].start()
+    for k in range(1, EARLY):
+        pltpu.make_async_copy(head[k], head[k], load_sem.at[2 + k]).wait()
+        for l in range(LANES):
+            convert(l, k, True)
+            copy(0, l, k).start()
+    for k in range(EARLY):
+        for l in range(LANES):
+            first(l, k, True)
     pltpu.make_async_copy(src, src, load_sem.at[1]).wait()
 
-    @pl.loop(1, max(chunks[l] + lag for _, _, l, lag in events))
+    @pl.loop(EARLY, max(chunks[l] + lag for _, _, l, lag in events))
     def _(t):
         for l in range(LANES):
 
@@ -217,7 +239,7 @@
 
         for _, s, l, lag in events:
 
-            @pl.when((t >= lag + (1 if s == 1 else 0)) & (t < chunks[l] + lag))
+            @pl.when((t >= lag + (EARLY if s == 1 else 0)) & (t < chunks[l] + lag))
             def _():
                 step(s, l, t - lag)
 
@@ -308,14 +330,15 @@
         out_specs=[pl.BlockSpec(memory_space=vmem)] * 2,
         scratch_shapes=[
             vmem((n_col, n_row, rows, w), gradients.dtype),
-            vmem((LANES, n_col, n_row, ROWS, COLS), gradients.dtype),
+            *[vmem((LANES, n_col, n_row, ROWS, COLS), gradients.dtype)] * EARLY,
             *[vmem((k, blocks, ROWS, COLS), F32) for k in chunks],
             *[vmem((k, blocks >> s, ROWS, COLS), F32) for k in chunks for s in range(bits + 1)],
             vmem((ROWS, wide), F32),
             vmem((1, wide), F32),
             vmem((devices, 1, wide), F32),
             smem(owner_offset.shape, jnp.int32),
-            dma((3,)),
+            dma((2 + EARLY,)),
+            dma((LANES,)),
             *[dma((bits + 1,)) for _ in chunks],
             *[dma((sum(ring),)) for ring in plan(bits)[1]],
             dma((2,)),
@@ -323,7 +346,7 @@
         compiler_params=pltpu.CompilerParams(
             collective_id=0, has_side_effects=True, vmem_limit_bytes=50 * 1024 * 1024
         ),
-    )(gradients.reshape(n_row, rows, width), owner_offset)
+    )(gradients.reshape(n_row, rows, width), pltpu.with_memory_space_constraint(owner_offset, pltpu.HBM))
     count = bucket_lengths.shape[0]
     clipped, rms = pl.pallas_call(
         functools.partial(scale, devices),

time: 93.5 us -> 92.7 us (level)
  no operation moved by 1% of the time
where the time goes in v3:
time: 92.7 us; the launch traced here: 92.6 us
  Pallas kernels  91.3 us (98%)
  between operations  1.31 us (1%)
    pallas_call x1, Pallas kernels, shards(): pl.pallas_call(functools.partial(kernel, n_row, n_col, bits), out_shape=(...  90.3 us

profile of v3, /device:TPU:0, one launch (start us, length us, event | category | flops | bytes accessed | tf_op | source)
XLA Modules:
  0.0 92.6 jit_solution(13781762668729665540)
XLA Ops:
  0.6 0.0 copy-start
  1.3 90.3 %shard_map.59 = (f32[128,1280]{1,0:T(8,128)S(1)}, f32[8,128]{1,0:T(8,128)S(1)}) custom-call(bf16[8,128,5120]{2,1,0:T(8,128)(2,1)} %bitcast.4, s32[8]{0:T(128)} %off_hbm.1), custom_call_target="tpu_custom_call" | custom-call | tf_op jit(solution)/shard_map/pallas_call | solution.py:323
  91.6 0.0 copy-done
  91.6 1.0 %shard_map.60 = (f32[128,1280]{1,0:T(8,128)}, f32[1,16]{1,0:T(1,128)}) custom-call(f32[128,1280]{1,0:T(8,128)S(1)} %get-tuple-element.6.avg_ref, f32[8,128]{1,0:T(8,128)S(1)} %get-tuple-element.7.stat_ref, s32[1,16]{1,0:T(1,128)S(1)} %bitcast.3, f32[1]{0:T(128)S(6)} %copy.6.clip_ref), custom_call_target="tpu_custom_call" | custom-call | tf_op jit(solution)/shard_map/pallas_call | solution.py:351
Async XLA Ops:
  0.6 90.9 %copy-start = (s32[16]{0:T(128)S(1)}, s32[16]{0:T(128)}, u32[]{:S(2)}) copy-start(s32[16]{0:T(128)} %param.5) | copy-start | bytes 196

commit v4 on v3

--- a/solution.py
+++ b/solution.py
@@ -42,12 +42,11 @@
 
 def kernel(n_row, n_col, bits, g_ref, off_hbm, out_ref, stat_ref, src, *rest):
     head, rest = rest[:EARLY], rest[EARLY:]
-    sent, rest = rest[:LANES], rest[LANES:]
-    sums, rest = [rest[l * (bits + 1) : (l + 1) * (bits + 1)] for l in range(LANES)], rest[LANES * (bits + 1) :]
+    sent, sums, rest = rest[0], rest[1 : bits + 2], rest[bits + 2 :]
     acc, mine, slots, off_ref, load_sem, begin, *rest = rest
-    sends, recvs, (both,) = rest[:LANES], rest[LANES : 2 * LANES], rest[2 * LANES :]
+    sends, *recvs, both = rest
     events, rings = plan(bits)
-    chunks = [s.shape[0] for s in sent]
+    chunks = split(sent.shape[0])
     blocks = 1 << bits
     devices = n_row * n_col
     _, _, rows, w = src.shape
@@ -106,9 +105,10 @@
 
     def copy(s, l, k):
         half = blocks >> s
-        a = sent[l].at[k] if s == 0 else sums[l][s - 1].at[k, pl.ds(half, half)]
+        u = bases[l] + k
+        a = sent.at[u] if s == 0 else sums[s - 1].at[u, pl.ds(half, half)]
         at = sum(rings[l][:s]) + k % rings[l][s]
-        return remote(a, sums[l][s].at[k], sends[l].at[s], recvs[l].at[at], target(s, l, k))
+        return remote(a, sums[s].at[u], sends.at[s], recvs[l].at[at], target(s, l, k))
 
     def spot(i, l, k):
         flips = {}
@@ -146,15 +146,16 @@
         def fill(i):
             r, yd = spot(i, l, k)
             for q in range(COLS // 128):
-                sent[l][k, i, :, q * 128 : (q + 1) * 128] = piece(l, k, start, r, yd * 2 + 1 - core, q)
+                sent[bases[l] + k, i, :, q * 128 : (q + 1) * 128] = piece(l, k, start, r, yd * 2 + 1 - core, q)
 
         each(lo, hi, fill)
 
     def halves(l):
         half = blocks // 2
+        u = bases[l]
         parts = ((half, begin.at[l]), (0, recvs[l].at[0]))
         return [
-            remote(sent[l].at[0, pl.ds(at, half)], sums[l][0].at[0, pl.ds(at, half)], sends[l].at[0], sem, target(0, l, 0))
+            remote(sent.at[u, pl.ds(at, half)], sums[0].at[u, pl.ds(at, half)], sends.at[0], sem, target(0, l, 0))
             for at, sem in parts
         ]
 
@@ -167,7 +168,7 @@
         def fold(i):
             r, yd = spot(i, l, k)
             for q in range(COLS // 128):
-                sums[l][0][k, i, :, q * 128 : (q + 1) * 128] += piece(l, k, start, r, yd * 2 + core, q)
+                sums[0][bases[l] + k, i, :, q * 128 : (q + 1) * 128] += piece(l, k, start, r, yd * 2 + core, q)
 
         each(blocks // 2, blocks, fold)
         copy(1, l, k).start()
@@ -181,18 +182,18 @@
 
         @pl.loop(half, 2 * half, unroll=min(2, half))
         def _(i):
-            sums[l][s - 1][k, i] += sums[l][s - 2][k, i]
+            sums[s - 1][bases[l] + k, i] += sums[s - 2][bases[l] + k, i]
 
         copy(s, l, k).start()
 
         @pl.loop(0, half, unroll=min(2, half))
         def _(i):
-            sums[l][s - 1][k, i] += sums[l][s - 2][k, i]
+            sums[s - 1][bases[l] + k, i] += sums[s - 2][bases[l] + k, i]
 
     def finish(l, k):
         copy(bits, l, k).wait_recv()
         top, base = unit(l, k)
-        v = (sums[l][bits][k, 0] + sums[l][bits - 1][k, 0]) * (1.0 / devices)
+        v = (sums[bits][bases[l] + k, 0] + sums[bits - 1][bases[l] + k, 0]) * (1.0 / devices)
         out_ref[pl.ds(pl.multiple_of(top, ROWS), ROWS), pl.ds(pl.multiple_of(base, COLS), COLS)] = v
         v = v * v
         total = v[:, 0:128]
@@ -257,11 +258,10 @@
     for mask in range(devices - 1, 0, -1):
         share(mask).start()
 
-    for l in range(LANES):
-        for s in range(bits + 1):
-            half = blocks >> s
-            a = sent[l] if s == 0 else sums[l][s - 1].at[:, pl.ds(half, half)]
-            pltpu.make_async_copy(a, a, sends[l].at[s]).wait()
+    for s in range(bits + 1):
+        half = blocks >> s
+        a = sent if s == 0 else sums[s - 1].at[:, pl.ds(half, half)]
+        pltpu.make_async_copy(a, a, sends.at[s]).wait()
 
     others = slots.at[pl.ds(0, devices - 1)]
     pltpu.make_async_copy(others, others, both.at[1]).wait()
@@ -316,7 +316,6 @@
     bits = devices.bit_length() - 2
     blocks = 1 << bits
     units = rows // ROWS * (w // COLS)
-    chunks = split(units)
     wide = -(-rows // 128) * 128
     vmem, smem = pltpu.VMEM, pltpu.SMEM
     dma = pltpu.SemaphoreType.DMA
@@ -331,15 +330,15 @@
         scratch_shapes=[
             vmem((n_col, n_row, rows, w), gradients.dtype),
             *[vmem((LANES, n_col, n_row, ROWS, COLS), gradients.dtype)] * EARLY,
-            *[vmem((k, blocks, ROWS, COLS), F32) for k in chunks],
-            *[vmem((k, blocks >> s, ROWS, COLS), F32) for k in chunks for s in range(bits + 1)],
+            vmem((units, blocks, ROWS, COLS), F32),
+            *[vmem((units, blocks >> s, ROWS, COLS), F32) for s in range(bits + 1)],
             vmem((ROWS, wide), F32),
             vmem((1, wide), F32),
             vmem((devices, 1, wide), F32),
             smem(owner_offset.shape, jnp.int32),
             dma((2 + EARLY,)),
             dma((LANES,)),
-            *[dma((bits + 1,)) for _ in chunks],
+            dma((bits + 1,)),
             *[dma((sum(ring),)) for ring in plan(bits)[1]],
             dma((2,)),
         ],

time: 92.7 us -> 92.7 us (level)
  no operation moved by 1% of the time
where the time goes in v4:
time: 92.7 us; the launch traced here: 92.5 us
  Pallas kernels  91.2 us (98%)
  between operations  1.31 us (1%)
    pallas_call x1, Pallas kernels, shards(): pl.pallas_call(functools.partial(kernel, n_row, n_col, bits), out_shape=(...  90.2 us

profile of v4, /device:TPU:0, one launch (start us, length us, event | category | flops | bytes accessed | tf_op | source)
XLA Modules:
  0.0 92.5 jit_solution(14130155145072003368)
XLA Ops:
  0.6 0.0 copy-start
  1.3 90.2 %shard_map.59 = (f32[128,1280]{1,0:T(8,128)S(1)}, f32[8,128]{1,0:T(8,128)S(1)}) custom-call(bf16[8,128,5120]{2,1,0:T(8,128)(2,1)} %bitcast.4, s32[8]{0:T(128)} %off_hbm.1), custom_call_target="tpu_custom_call" | custom-call | tf_op jit(solution)/shard_map/pallas_call | solution.py:322
  91.5 0.0 copy-done
  91.5 1.0 %shard_map.60 = (f32[128,1280]{1,0:T(8,128)}, f32[1,16]{1,0:T(1,128)}) custom-call(f32[128,1280]{1,0:T(8,128)S(1)} %get-tuple-element.6.avg_ref, f32[8,128]{1,0:T(8,128)S(1)} %get-tuple-element.7.stat_ref, s32[1,16]{1,0:T(1,128)S(1)} %bitcast.3, f32[1]{0:T(128)S(6)} %copy.6.clip_ref), custom_call_target="tpu_custom_call" | custom-call | tf_op jit(solution)/shard_map/pallas_call | solution.py:350
Async XLA Ops:
  0.6 90.8 %copy-start = (s32[16]{0:T(128)S(1)}, s32[16]{0:T(128)}, u32[]{:S(2)}) copy-start(s32[16]{0:T(128)} %param.5) | copy-start | bytes 196
